TPU v7x, 32 devices: a whole 2x2x4 slice. The times are simulated.
32 devices in a mesh: groups: 2 (over y), bank: 4 (over x, core), tensor: 4 (over z).
Axes of the slice: x: 2, y: 2, z: 4, core: 2. Of those that a mesh axis runs over, the one named last changes fastest.
Arguments:
- latest_activations: bfloat16 [64, 8192], P(('groups', 'bank'), 'tensor'), parts along dimension 0, may hold values from -6 to 6
- layer_normalizer_gains_table: bfloat16 [8192], replicated, may hold values from 0.5 to 1.5
- asker_projection: bfloat16 [8192, 8192], P('bank', 'tensor'), may hold values from -0.0625 to 0.0625
- memory_projection_stack: bfloat16 [2, 8192, 1024], P(None, 'bank', 'tensor'), may hold values from -0.0625 to 0.0625
- narrowing_factors: bfloat16 [128, 48, 8192], P('bank', None, 'tensor'), may hold values from -0.0625 to 0.0625
- widening_factors_asker: bfloat16 [128, 16, 8192], P('bank', None, 'tensor'), may hold values from -1.5 to 1.5
- widening_factors_memory: bfloat16 [128, 2, 16, 1024], P('bank', None, None, 'tensor'), may hold values from -1.5 to 1.5
- tweak_for_stream: int32 [64], P(('groups', 'bank')), parts along dimension 0, may hold values from 0 to 127
- stream_offsets: int32 [64], P(('groups', 'bank')), parts along dimension 0, may hold values from 2 to 1024
- saved_rotated_addresses: bfloat16 [64, 1024, 8, 128], P(('groups', 'bank'), None, 'tensor'), parts along dimension 0, may hold values from -1200 to 1200
- saved_contents: bfloat16 [64, 1024, 8, 128], P(('groups', 'bank'), None, 'tensor'), parts along dimension 0, may hold values from -6 to 6
Outputs:
- attention: bfloat16 [64, 8192], P(('groups', 'bank'), 'tensor'), parts along dimension 0
There are 2 independent parts, one for each index of `groups`. A program takes and returns all parts, laid end to end along the dimension named above; an argument that names none is the same for every part. Nothing has to cross between parts.
All inputs are finite; a program needn't handle non-finite values.
Results may differ from a plain program's by a relative error of at most 0.0095.
The roundings to bfloat16 on the way count: a program that leaves them out, or rounds other values in their place, can miss the bound.
Values may be sent and summed in bfloat16 or wider, within the bound.
No kernel may reach another device: no remote copies, remote signals or barrier semaphores. Data moves between devices by JAX's collectives and lax.ppermute only.
A program may use at most 64 MiB of HBM per device.

v0:
```python
import math
import jax
import jax.numpy as jnp
from jax import lax
from jax.sharding import PartitionSpec as P

rope_base = 500000.0
tweak_strength = 2.0
epsilon = 1e-05


def rotate(values, positions):
    half_dim = values.shape[-1] // 2
    freqs = rope_base ** (-(jnp.arange(half_dim, dtype=jnp.float32) * 2.0) / values.shape[-1])
    angles = positions.astype(jnp.float32)[:, None] * freqs[None, :]
    cosine = jnp.cos(angles)[:, None, :]
    sine_part = jnp.sin(angles)[:, None, :]
    front_half = values[..., :half_dim]
    back_half = values[..., half_dim:]
    return jnp.concatenate(
        [front_half * cosine - back_half * sine_part, back_half * cosine + front_half * sine_part],
        axis=-1,
    )


def attend_local(
    probe_vectors, current_lookup_vectors, values_new, cache_keys, cache_values, stream_offsets
):
    reciprocal_sqrt_dim = 1.0 / math.sqrt(probe_vectors.shape[-1])
    scores = (
        jnp.einsum("bkgd,bpkd->bkgp", probe_vectors, cache_keys, preferred_element_type=jnp.float32)
        * reciprocal_sqrt_dim
    )
    self_logit = (
        jnp.einsum(
            "atcj,atj->atc",
            probe_vectors,
            current_lookup_vectors,
            preferred_element_type=jnp.float32,
        )
        * reciprocal_sqrt_dim
    )
    positions = lax.broadcasted_iota(jnp.int32, scores.shape, 3)
    live_mask = positions < stream_offsets[:, None, None, None]
    peak_score = jnp.maximum(jnp.max(jnp.where(live_mask, scores, -jnp.inf), axis=-1), self_logit)
    expo = jnp.where(live_mask, jnp.exp(scores - peak_score[..., None]), 0.0)
    own_expo = jnp.exp(self_logit - peak_score)
    total = jnp.sum(expo, axis=-1) + own_expo
    weights = (expo / total[..., None]).astype(jnp.bfloat16)
    own_weight = (own_expo / total).astype(jnp.bfloat16)
    mixed = jnp.einsum("bkgp,bpkd->bkgd", weights, cache_values, preferred_element_type=jnp.float32)
    return (
        mixed
        + own_weight.astype(jnp.float32)[..., None] * values_new.astype(jnp.float32)[:, :, None, :]
    )


def shards(
    latest_activations,
    layer_normalizer_gains_table,
    asker_projection,
    memory_projection_stack,
    narrowing_factors,
    widening_factors_asker,
    widening_factors_memory,
    tweak_for_stream,
    stream_offsets,
    saved_rotated_addresses,
    saved_contents,
):
    joined_rows = lax.all_gather(latest_activations, "tensor", axis=1, tiled=True)
    tok_float = joined_rows.astype(jnp.float32)
    mean_square = jnp.mean(tok_float * tok_float, axis=1, keepdims=True)
    normed = (
        tok_float
        * lax.rsqrt(mean_square + epsilon)
        * layer_normalizer_gains_table.astype(jnp.float32)[None, :]
    ).astype(jnp.bfloat16)
    n_bank = lax.axis_size("bank")
    n_tensor = lax.axis_size("tensor")
    bank_index = lax.axis_index("bank")
    tensor_index = lax.axis_index("tensor")
    model_width = normed.shape[1]
    piece_bank = model_width // n_bank
    piece_tensor = model_width // n_tensor
    row_count = latest_activations.shape[0]
    every_row, all_ids = (
        lax.all_gather(normed, "bank", axis=0, tiled=True),
        lax.all_gather(tweak_for_stream, "bank", axis=0, tiled=True),
    )
    base_input = lax.dynamic_slice_in_dim(every_row, bank_index * piece_bank, piece_bank, 1)
    hidden_after_rmsnorm = lax.dynamic_slice_in_dim(
        every_row, tensor_index * piece_tensor, piece_tensor, 1
    )
    sequences_on_device = narrowing_factors.shape[0]
    low_dim_extent = widening_factors_asker.shape[1]
    owned_ids = bank_index * sequences_on_device + jnp.arange(sequences_on_device, dtype=jnp.int32)
    picked = all_ids[None, :] == owned_ids[:, None]
    projected_low_vector = jnp.einsum(
        "omk,lk->oml", narrowing_factors, hidden_after_rmsnorm, preferred_element_type=jnp.float32
    )
    inner_part = jnp.sum(jnp.where(picked[:, None, :], projected_low_vector, 0.0), axis=0)
    inner_sum = lax.psum(inner_part, "tensor")
    inner_low = inner_sum.astype(jnp.bfloat16)
    pick_low = picked.astype(jnp.bfloat16)

    def spread(rank_block):
        expanded = pick_low[:, None, :] * rank_block[None, :, :]
        return expanded.reshape(sequences_on_device * low_dim_extent, rank_block.shape[1])

    probe_proj_span = asker_projection.shape[1]
    shared_proj_span = memory_projection_stack.shape[2]
    probe_correction = jnp.einsum(
        "cs,co->so",
        spread(inner_low[0:low_dim_extent]),
        widening_factors_asker.reshape(sequences_on_device * low_dim_extent, probe_proj_span),
        preferred_element_type=jnp.float32,
    )
    lookup_correction = jnp.einsum(
        "cs,co->so",
        spread(inner_low[low_dim_extent : 2 * low_dim_extent]),
        widening_factors_memory[:, 0].reshape(
            sequences_on_device * low_dim_extent, shared_proj_span
        ),
        preferred_element_type=jnp.float32,
    )
    payload_correction = jnp.einsum(
        "cs,co->so",
        spread(inner_low[2 * low_dim_extent : 3 * low_dim_extent]),
        widening_factors_memory[:, 1].reshape(
            sequences_on_device * low_dim_extent, shared_proj_span
        ),
        preferred_element_type=jnp.float32,
    )
    tweak_contribution = tweak_strength * jnp.concatenate(
        [probe_correction, lookup_correction, payload_correction], axis=1
    )
    untouched_share = lax.psum_scatter(
        jnp.concatenate(
            [
                jnp.dot(base_input, asker_projection, preferred_element_type=jnp.float32),
                jnp.dot(base_input, memory_projection_stack[0], preferred_element_type=jnp.float32),
                jnp.dot(base_input, memory_projection_stack[1], preferred_element_type=jnp.float32),
            ],
            axis=1,
        ),
        "bank",
        scatter_dimension=0,
        tiled=True,
    )
    accumulated_total = untouched_share + lax.psum_scatter(
        tweak_contribution, "bank", scatter_dimension=0, tiled=True
    )
    head_dim = saved_rotated_addresses.shape[3]
    kv_heads = saved_rotated_addresses.shape[2]
    q_heads = probe_proj_span // head_dim
    query_part = accumulated_total[:, 0:probe_proj_span].reshape(row_count, q_heads, head_dim)
    key_part = accumulated_total[:, probe_proj_span : probe_proj_span + shared_proj_span].reshape(
        row_count, kv_heads, head_dim
    )
    value_part = accumulated_total[
        :, probe_proj_span + shared_proj_span : probe_proj_span + 2 * shared_proj_span
    ].reshape(row_count, kv_heads, head_dim)
    q_rot = rotate(query_part, stream_offsets).astype(jnp.bfloat16)
    k_new = rotate(key_part, stream_offsets).astype(jnp.bfloat16)
    v_new = value_part.astype(jnp.bfloat16)
    probe_vectors = q_rot.reshape(row_count, kv_heads, q_heads // kv_heads, head_dim)
    mixed = attend_local(
        probe_vectors, k_new, v_new, saved_rotated_addresses, saved_contents, stream_offsets
    )
    return mixed.reshape(row_count, probe_proj_span).astype(jnp.bfloat16)


def solution(mesh):
    placed = (
        P(("groups", "bank"), "tensor"),
        P(),
        P("bank", "tensor"),
        P(None, "bank", "tensor"),
        P("bank", None, "tensor"),
        P("bank", None, "tensor"),
        P("bank", None, None, "tensor"),
        P(("groups", "bank")),
        P(("groups", "bank")),
        P(("groups", "bank"), None, "tensor", None),
        P(("groups", "bank"), None, "tensor", None),
    )
    return jax.shard_map(
        shards,
        mesh=mesh,
        in_specs=placed,
        out_specs=P(("groups", "bank"), "tensor"),
        check_vma=False,
    )
```

profile of v0, /device:TPU:0, one launch (start us, length us, event | category | flops | bytes accessed | tf_op | source)
XLA Modules:
  0.0 105.4 jit_solution(16486017365840379025)
XLA Ops:
  6.5 15.4 %all_gather.9 = bf16[8,8192]{1,0:T(8,128)(2,1)S(1)} all-gather(bf16[8,2048]{1,0:T(8,128)(2,1)} %param.11), channel_id=1, replica_groups=mesh['groups'=2,'bank'=4,'tensor'=4] {'tensor'}, dimensions={1}, use_global_device_ids=true | all-gather | bytes 163840 | tf_op jit(solution)/shard_map/all_gather | solution.py:71
  22.0 0.7 convert_element_type.58
  22.7 0.2 fusion.25
  23.0 7.2 %all_gather.10 = bf16[32,8192]{1,0:T(8,128)(2,1)S(1)} all-gather(bf16[8,8192]{1,0:T(8,128)(2,1)S(1)} %fusion.27), channel_id=1, replica_groups=mesh['groups'=2,'bank'=4,'tensor'=4] {'bank'}, dimensions={0}, use_global_device_ids=true | all-gather | bytes 655360 | tf_op jit(solution)/shard_map/all_gather | solution.py:88
  30.2 1.5 %fusion.18 = f32[32,256]{1,0:T(8,128)S(1)} fusion(bf16[2,2048,256]{2,1,0:T(8,128)(2,1)} %param.14, bf16[32,8192]{1,0:T(8,128)(2,1)S(1)} %all_gather.10, s32[]{:T(128)S(6)} %select_n.17), kind=kOutput, calls=%fused_computation.12 | convolution fusion | flops 33554432 | bytes 1212420 | tf_op jit(solution)/shard_map/dot_general | solution.py:143
  31.7 1.5 %fusion.20 = f32[32,256]{1,0:T(8,128)S(1)} fusion(bf16[2,2048,256]{2,1,0:T(8,128)(2,1)} %param.14, bf16[32,8192]{1,0:T(8,128)(2,1)S(1)} %all_gather.10, s32[]{:T(128)S(6)} %select_n.17), kind=kOutput, calls=%fused_computation.14 | convolution fusion | flops 33554432 | bytes 1212420 | tf_op jit(solution)/shard_map/dot_general | solution.py:142
  33.2 4.9 %fusion.37 = f32[32,2048]{1,0:T(8,128)S(1)} fusion(bf16[2048,2048]{1,0:T(8,128)(2,1)} %param.13, bf16[32,8192]{1,0:T(8,128)(2,1)S(1)} %all_gather.10, s32[]{:T(128)S(6)} %select_n.17), kind=kOutput, calls=%fused_computation.39 | convolution fusion | flops 268435456 | bytes 8781828 | tf_op jit(solution)/shard_map/dot_general | solution.py:141
  38.2 0.6 dynamic-slice
  39.4 0.2 dynamic-update-slice
  39.7 4.3 %all-reduce = s32[32]{0:T(128)S(1)} all-reduce(s32[32]{0:T(128)S(1)} %dynamic-update-slice), channel_id=1, replica_groups=mesh['groups'=2,'bank'=4,'tensor'=4] {'bank'}, use_global_device_ids=true, to_apply=%add | all-reduce | flops 32 | bytes 256
  44.0 6.5 %fusion.8 = f32[48,32]{0,1:T(8,128)S(1)} fusion(bf16[32,48,2048]{2,1,0:T(8,128)(2,1)} %param.15, pred[32,32]{1,0:T(8,128)(4,1)S(1)} %get-tuple-element.21, bf16[32,8192]{1,0:T(8,128)(2,1)S(1)} %all_gather.10, s32[]{:T(128)S(6)} %select_n.18), kind=kOutput, calls=%fused_computation.8 | convolution fusion | flops 201423360 | bytes 6432772 | tf_op jit(solution)/shard_map/omk,lk->oml/dot_general | solution.py:99
  50.5 19.1 %psum.7 = bf16[48,32]{0,1:T(8,128)(2,1)S(1)} all-reduce(f32[48,32]{0,1:T(8,128)S(1)} %fusion.8), channel_id=1, replica_groups=mesh['groups'=2,'bank'=4,'tensor'=4] {'tensor'}, use_global_device_ids=true, to_apply=%region_3.4 | all-reduce | flops 1536 | bytes 9216 | tf_op jit(solution)/shard_map/psum | solution.py:103
  70.2 0.2 fusion.57
  70.4 0.5 convolution_bitcast_fusion
  70.9 0.8 maximum_add_fusion
  71.8 18.3 %reduce-scatter.2.cloned.1.call-done = f32[8,2560]{1,0:T(8,128)} async-done(((f32[32,2560]{1,0:T(8,128)}), f32[8,2560]{1,0:T(8,128)}) %reduce-scatter.2.cloned.1.call-update) | async-done | bytes 81936 | tf_op jit(solution)/shard_map/reduce_scatter | solution.py:138
  90.2 1.0 slice_bitcast_fusion
  91.3 0.9 slice_bitcast_fusion.1
  92.4 3.5 %select_reduce_fusion = (f32[8,2,8]{2,1,0:T(2,128)S(1)}, f32[8,2,8,1024]{3,2,1,0:T(8,128)S(1)}) fusion(s32[8]{0:T(128)S(1)} %copy-done.2, bf16[8,1024,2,128]{3,2,1,0:T(2,128)(2,1)} %param.20, bf16[8,2,8,64]{3,2,1,0:T(8,128)(2,1)S(1)} %get-tuple-element.24, bf16[8,2,8,64]{3,2,1,0:T(8,128)(2,1)S(1)} %get-tuple-element.25), kind=kOutput, calls=%fused_computation.20 | convolution fusion | flops 34144128 | bytes 4751904 | tf_op jit(solution)/shard_map/bkgd,bpkd->bkgp/dot_general | solution.py:31
  95.9 0.2 fusion.41
  96.1 0.3 fusion.24
  96.4 0.7 fusion.44
  97.1 0.8 fusion.15
  97.9 0.6 copy.56
  (36 shorter events, 1.2 us)
Async XLA Ops:
  6.5 63.9 %copy-start = (bf16[32,16,2048]{2,1,0:T(8,128)(2,1)S(1)}, bf16[32,16,2048]{2,1,0:T(8,128)(2,1)}, u32[]{:S(2)}) copy-start(bf16[32,16,2048]{2,1,0:T(8,128)(2,1)} %param.16) | copy-start | bytes 6291460
  6.5 83.7 %reduce-scatter.2.cloned.1.call-start = ((), (), s32[]{:S(2)}) async-start(), calls=%async_computation.1 | async-start | bytes 409600 | tf_op jit(solution)/shard_map/reduce_scatter | solution.py:138
  33.2 5.0 %copy-start.5 = (u32[32]{0:T(128)S(1)}, u32[32]{0:T(128)}, u32[]{:S(2)}) copy-start(u32[32]{0:T(128)} %constant.39) | copy-start | bytes 388
  33.2 6.2 %copy-start.4 = (s32[8]{0:T(128)S(1)}, s32[8]{0:T(128)}, u32[]{:S(2)}) copy-start(s32[8]{0:T(128)} %param.18) | copy-start | bytes 100
  38.1 31.7 %copy-start.1 = (bf16[32,2,16,256]{3,2,1,0:T(8,128)(2,1)S(1)}, bf16[32,2,16,256]{3,2,1,0:T(8,128)(2,1)}, u32[]{:S(2)}) copy-start(bf16[32,2,16,256]{3,2,1,0:T(8,128)(2,1)} %param.17) | copy-start | bytes 1572868
  50.5 21.2 %copy-start.2 = (s32[8]{0:T(128)S(1)}, s32[8]{0:T(128)}, u32[]{:S(2)}) copy-start(s32[8]{0:T(128)} %param.19) | copy-start | bytes 100
  90.2 6.9 %copy-start.3 = (bf16[8,1024,2,128]{3,2,1,0:T(2,128)(2,1)S(1)}, bf16[8,1024,2,128]{3,2,1,0:T(2,128)(2,1)}, u32[]{:S(2)}) copy-start(bf16[8,1024,2,128]{3,2,1,0:T(2,128)(2,1)} %param.21) | copy-start | bytes 12582916
Sparse Core Ops, SparseCore 0:
  71.8 18.3 reduce-scatter.1
where the time goes:
time: 106 us; the launch traced here: 105 us
  blocking collectives  46 us (43%)
  matrix products  19.8 us (19%)
  waiting for transfers between devices  18.4 us (17%)
  between operations  14.2 us (13%)
  local copies, waits for them, and re-layouts  3.78 us (4%)
  other arithmetic  3.25 us (3%)
    psum x1, blocking collectives, shards(): inner_sum = lax.psum(inner_part, 'tensor')  19.1 us
    reduce_scatter x1, waiting for transfers between devices, shards(): lax.psum_scatter(jnp.concatenate([jnp.dot(base_input, asker_projection, p...  18.3 us
    all_gather x1, blocking collectives, shards(): lax.all_gather(latest_activations, 'tensor', axis=1, tiled=True)  15.4 us
    all_gather x1, blocking collectives, shards(): lax.all_gather(normed, 'bank', axis=0, tiled=True)  7.17 us
    dot_general x1, matrix products, shards(): jnp.einsum('omk,lk->oml', narrowing_factors, hidden_after_rmsnorm, prefer...  6.49 us
    dot_general x1, matrix products, shards(): jnp.dot(base_input, asker_projection, preferred_element_type=jnp.float32)  4.93 us
    unnamed x1, blocking collectives  4.26 us
    dot_general x1, matrix products, attend_local(): jnp.einsum('bkgd,bpkd->bkgp', probe_vectors, cache_keys, preferred_elemen...  3.5 us
  transfers between devices with their start and end apart: 1, of which 1 were waited for; matrix products, arithmetic and copies ran while one was open for 0% of the time, Pallas kernels for 0%

commit v1 on v0

--- a/solution.py
+++ b/solution.py
@@ -7,6 +7,14 @@
 rope_base = 500000.0
 tweak_strength = 2.0
 epsilon = 1e-05
+
+
+def added_up(block, name):
+    size, total = (lax.axis_size(name), block)
+    for far in [1 << k for k in range(size.bit_length() - 1)]:
+        swap = [(i, i ^ far) for i in range(size)]
+        total = total + lax.ppermute(total, name, swap)
+    return total
 
 
 def rotate(values, positions):
@@ -100,7 +108,7 @@
         "omk,lk->oml", narrowing_factors, hidden_after_rmsnorm, preferred_element_type=jnp.float32
     )
     inner_part = jnp.sum(jnp.where(picked[:, None, :], projected_low_vector, 0.0), axis=0)
-    inner_sum = lax.psum(inner_part, "tensor")
+    inner_sum = added_up(inner_part, "tensor")
     inner_low = inner_sum.astype(jnp.bfloat16)
     pick_low = picked.astype(jnp.bfloat16)
 

time: 106 us -> 95.3 us (0.90)
  blocking collectives: 46 us -> 26.8 us
  starting transfers between devices: 0.01 us -> 4.4 us
  waiting for transfers between devices: 18.4 us -> 22.4 us
  local copies, waits for them, and re-layouts: 3.78 us -> 5.04 us
    psum x1 -> x0, blocking collectives: 19.1 us -> none  [shards(): inner_sum = lax.psum(inner_part, 'tensor')]
    ppermute x0 -> x2, starting transfers between devices: none -> 4.39 us  [added_up(): total = total + lax.ppermute(total, name, swap)]
    ppermute x0 -> x2, waiting for transfers between devices: none -> 2.2 us  [added_up(): total = total + lax.ppermute(total, name, swap)]
    reduce_scatter x1, waiting for transfers between devices: 18.3 us -> 20.2 us  [shards(): lax.psum_scatter(jnp.concatenate([jnp.dot(base_input, asker_projection, p...]
    unnamed x16 -> x14, local copies, waits for them, and re-layouts: 1.5 us -> 2.77 us
    dot_general x1, matrix products: 1.51 us -> 0.28 us  [shards(): jnp.dot(base_input, memory_projection_stack[0], preferred_element_type=jn...]
  transfers between devices with their start and end apart: 1 -> 3, of which waited for: 1 -> 2; matrix products, arithmetic and copies ran while one was open for 0% -> 7% of each run, Pallas kernels for 0% -> 0%
where the time goes in v1:
time: 95.3 us; the launch traced here: 94.9 us
  blocking collectives  26.8 us (28%)
  waiting for transfers between devices  22.4 us (24%)
  matrix products  18.8 us (20%)
  between operations  14.2 us (15%)
  local copies, waits for them, and re-layouts  5.04 us (5%)
  starting transfers between devices  4.4 us (5%)
  other arithmetic  3.27 us (3%)
    reduce_scatter x1, waiting for transfers between devices, shards(): lax.psum_scatter(jnp.concatenate([jnp.dot(base_input, asker_projection, p...  20.2 us
    all_gather x1, blocking collectives, shards(): lax.all_gather(latest_activations, 'tensor', axis=1, tiled=True)  15.4 us
    all_gather x1, blocking collectives, shards(): lax.all_gather(normed, 'bank', axis=0, tiled=True)  7.17 us
    dot_general x1, matrix products, shards(): jnp.einsum('omk,lk->oml', narrowing_factors, hidden_after_rmsnorm, prefer...  6.49 us
    dot_general x1, matrix products, shards(): jnp.dot(base_input, asker_projection, preferred_element_type=jnp.float32)  5.08 us
    ppermute x2, starting transfers between devices, added_up(): total = total + lax.ppermute(total, name, swap)  4.39 us
    unnamed x1, blocking collectives  4.26 us
    dot_general x1, matrix products, attend_local(): jnp.einsum('bkgd,bpkd->bkgp', probe_vectors, cache_keys, preferred_elemen...  3.5 us
  transfers between devices with their start and end apart: 3, of which 2 were waited for; matrix products, arithmetic and copies ran while one was open for 7% of the time, Pallas kernels for 0%

profile of v1, /device:TPU:0, one launch (start us, length us, event | category | flops | bytes accessed | tf_op | source)
XLA Modules:
  0.0 94.9 jit_solution(10689348180470847986)
XLA Ops:
  6.5 15.4 %all_gather.9 = bf16[8,8192]{1,0:T(8,128)(2,1)S(1)} all-gather(bf16[8,2048]{1,0:T(8,128)(2,1)} %param.11), channel_id=1, replica_groups=mesh['groups'=2,'bank'=4,'tensor'=4] {'tensor'}, dimensions={1}, use_global_device_ids=true | all-gather | bytes 163840 | tf_op jit(solution)/shard_map/all_gather | solution.py:79
  22.0 0.7 convert_element_type.58
  23.0 7.2 %all_gather.10 = bf16[32,8192]{1,0:T(8,128)(2,1)S(1)} all-gather(bf16[8,8192]{1,0:T(8,128)(2,1)S(1)} %fusion.27), channel_id=1, replica_groups=mesh['groups'=2,'bank'=4,'tensor'=4] {'bank'}, dimensions={0}, use_global_device_ids=true | all-gather | bytes 655360 | tf_op jit(solution)/shard_map/all_gather | solution.py:96
  30.2 1.2 %dynamic-slice = u32[1]{0:T(128)} dynamic-slice(u32[32]{0:T(128)} %constant.39, u32[]{:T(128)S(6)} %add.62), dynamic_slice_sizes={1} | dynamic-slice | bytes 12
  32.1 0.9 dynamic-update-slice
  32.9 4.3 %all-reduce = s32[32]{0:T(128)S(1)} all-reduce(s32[32]{0:T(128)S(1)} %dynamic-update-slice), channel_id=1, replica_groups=mesh['groups'=2,'bank'=4,'tensor'=4] {'bank'}, use_global_device_ids=true, to_apply=%add | all-reduce | flops 32 | bytes 256
  37.3 6.5 %fusion.8 = f32[48,32]{0,1:T(8,128)S(1)} fusion(bf16[32,48,2048]{2,1,0:T(8,128)(2,1)} %param.15, pred[32,32]{1,0:T(8,128)(4,1)S(1)} %get-tuple-element.21, bf16[32,8192]{1,0:T(8,128)(2,1)S(1)} %all_gather.10, s32[]{:T(128)S(6)} %select_n.18), kind=kOutput, calls=%fused_computation.8 | convolution fusion | flops 201423360 | bytes 6432772 | tf_op jit(solution)/shard_map/omk,lk->oml/dot_general | solution.py:107
  43.8 1.9 %collective-permute-start = (f32[48,32]{0,1:T(8,128)S(1)}, f32[48,32]{0,1:T(8,128)S(1)}, u32[]{:S(2)}, u32[]{:S(2)}) collective-permute-start(f32[48,32]{0,1:T(8,128)S(1)} %fusion.8), channel_id=1, source_target_pairs={{0,1},{1,0},{2,3},{3,2},{4,5},{5,4},{6,7},{7,6},{8,9},{9,8},{10,11... | collective-permute-start | bytes 18440 | tf_op jit(solution)/shard_map/ppermute | solution.py:16
  45.7 1.5 %fusion.18 = f32[32,256]{1,0:T(8,128)S(1)} fusion(bf16[2,2048,256]{2,1,0:T(8,128)(2,1)} %param.14, bf16[32,8192]{1,0:T(8,128)(2,1)S(1)} %all_gather.10, s32[]{:T(128)S(6)} %select_n.17), kind=kOutput, calls=%fused_computation.12 | convolution fusion | flops 33554432 | bytes 1212420 | tf_op jit(solution)/shard_map/dot_general | solution.py:151
  47.2 5.1 %fusion.37 = f32[32,2048]{1,0:T(8,128)S(1)} fusion(bf16[2048,2048]{1,0:T(8,128)(2,1)} %param.13, bf16[32,8192]{1,0:T(8,128)(2,1)S(1)} %all_gather.10, s32[]{:T(128)S(6)} %select_n.17), kind=kOutput, calls=%fused_computation.39 | convolution fusion | flops 268435456 | bytes 8781828 | tf_op jit(solution)/shard_map/dot_general | solution.py:149
  52.3 0.3 fusion.20
  52.6 2.5 %collective-permute-start.1 = (f32[48,32]{0,1:T(8,128)S(1)}, f32[48,32]{0,1:T(8,128)S(1)}, u32[]{:S(2)}, u32[]{:S(2)}) collective-permute-start(f32[48,32]{0,1:T(8,128)S(1)} %add.54), channel_id=1, source_target_pairs={{0,2},{1,3},{2,0},{3,1},{4,6},{5,7},{6,4},{7,5},{8,10},{9,11},{10,... | collective-permute-start | bytes 18440 | tf_op jit(solution)/shard_map/ppermute | solution.py:16
  55.1 2.2 %collective-permute-done.1 = f32[48,32]{0,1:T(8,128)S(1)} collective-permute-done((f32[48,32]{0,1:T(8,128)S(1)}, f32[48,32]{0,1:T(8,128)S(1)}, u32[]{:S(2)}, u32[]{:S(2)}) %collective-permute-start.1) | collective-permute-done | bytes 6176 | tf_op jit(solution)/shard_map/ppermute | solution.py:16
  58.1 0.5 convolution_bitcast_fusion
  58.6 0.8 maximum_add_fusion
  59.5 20.2 %reduce-scatter.2.cloned.1.call-done = f32[8,2560]{1,0:T(8,128)} async-done(((f32[32,2560]{1,0:T(8,128)}), f32[8,2560]{1,0:T(8,128)}) %reduce-scatter.2.cloned.1.call-update) | async-done | bytes 81936 | tf_op jit(solution)/shard_map/reduce_scatter | solution.py:146
  79.7 1.0 %slice_bitcast_fusion = f32[8,16,128]{2,0,1:T(8,128)S(1)} fusion(f32[8,2560]{1,0:T(8,128)} %reduce-scatter.2.cloned.1.call-done), kind=kLoop, calls=%fused_computation.41 | loop fusion | bytes 131072 | tf_op jit(solution)/shard_map/reshape | solution.py:165
  80.8 0.9 slice_bitcast_fusion.1
  81.8 3.5 %select_reduce_fusion = (f32[8,2,8]{2,1,0:T(2,128)S(1)}, f32[8,2,8,1024]{3,2,1,0:T(8,128)S(1)}) fusion(s32[8]{0:T(128)S(1)} %copy-done.3, bf16[8,1024,2,128]{3,2,1,0:T(2,128)(2,1)} %param.20, bf16[8,2,8,64]{3,2,1,0:T(8,128)(2,1)S(1)} %get-tuple-element.24, bf16[8,2,8,64]{3,2,1,0:T(8,128)(2,1)S(1)} %get-tuple-element.25), kind=kOutput, calls=%fused_computation.20 | convolution fusion | flops 34144128 | bytes 4751904 | tf_op jit(solution)/shard_map/bkgd,bpkd->bkgp/dot_general | solution.py:39
  85.3 0.2 fusion.41
  85.6 0.3 fusion.24
  85.9 0.7 fusion.44
  86.6 0.8 fusion.15
  87.4 0.6 copy.56
  (39 shorter events, 1.6 us)
Async XLA Ops:
  6.5 51.6 %copy-start = (bf16[32,16,2048]{2,1,0:T(8,128)(2,1)S(1)}, bf16[32,16,2048]{2,1,0:T(8,128)(2,1)}, u32[]{:S(2)}) copy-start(bf16[32,16,2048]{2,1,0:T(8,128)(2,1)} %param.16) | copy-start | bytes 6291460
  6.5 73.1 %reduce-scatter.2.cloned.1.call-start = ((), (), s32[]{:S(2)}) async-start(), calls=%async_computation.1 | async-start | bytes 409600 | tf_op jit(solution)/shard_map/reduce_scatter | solution.py:146
  43.8 8.8 %collective-permute-start = (f32[48,32]{0,1:T(8,128)S(1)}, f32[48,32]{0,1:T(8,128)S(1)}, u32[]{:S(2)}, u32[]{:S(2)}) collective-permute-start(f32[48,32]{0,1:T(8,128)S(1)} %fusion.8), channel_id=1, source_target_pairs={{0,1},{1,0},{2,3},{3,2},{4,5},{5,4},{6,7},{7,6},{8,9},{9,8},{10,11... | collective-permute-start | bytes 18440 | tf_op jit(solution)/shard_map/ppermute | solution.py:16
  47.2 5.1 %copy-start.1 = (bf16[2,2048,256]{2,1,0:T(8,128)(2,1)S(1)}, bf16[2,2048,256]{2,1,0:T(8,128)(2,1)}, u32[]{:S(2)}) copy-start(bf16[2,2048,256]{2,1,0:T(8,128)(2,1)} %param.14) | copy-start | bytes 6291460
  47.2 7.9 %copy-start.2 = (bf16[32,2,16,256]{3,2,1,0:T(8,128)(2,1)S(1)}, bf16[32,2,16,256]{3,2,1,0:T(8,128)(2,1)}, u32[]{:S(2)}) copy-start(bf16[32,2,16,256]{3,2,1,0:T(8,128)(2,1)} %param.17) | copy-start | bytes 1572868
  52.3 7.1 %copy-start.3 = (s32[8]{0:T(128)S(1)}, s32[8]{0:T(128)}, u32[]{:S(2)}) copy-start(s32[8]{0:T(128)} %param.19) | copy-start | bytes 100
  52.6 4.7 %collective-permute-start.1 = (f32[48,32]{0,1:T(8,128)S(1)}, f32[48,32]{0,1:T(8,128)S(1)}, u32[]{:S(2)}, u32[]{:S(2)}) collective-permute-start(f32[48,32]{0,1:T(8,128)S(1)} %add.54), channel_id=1, source_target_pairs={{0,2},{1,3},{2,0},{3,1},{4,6},{5,7},{6,4},{7,5},{8,10},{9,11},{10,... | collective-permute-start | bytes 18440 | tf_op jit(solution)/shard_map/ppermute | solution.py:16
  79.7 6.9 %copy-start.4 = (bf16[8,1024,2,128]{3,2,1,0:T(2,128)(2,1)S(1)}, bf16[8,1024,2,128]{3,2,1,0:T(2,128)(2,1)}, u32[]{:S(2)}) copy-start(bf16[8,1024,2,128]{3,2,1,0:T(2,128)(2,1)} %param.21) | copy-start | bytes 12582916
Sparse Core Ops, SparseCore 0:
  59.5 20.1 reduce-scatter.1
